TPU v7x, 32 devices: a whole 2x2x4 slice. The times are simulated.
32 devices in a mesh: gx: 4 (over z), gy: 2 (over y), gz: 4 (over x, core).
Axes of the slice: x: 2, y: 2, z: 4, core: 2. Of those that a mesh axis runs over, the one named last changes fastest.
Arguments:
- coords: float32 [3, 65536], P(None, ('gx', 'gy', 'gz')), may hold values from 0 to 3
- anchor: float32 [3, 65536], P(None, ('gx', 'gy', 'gz')), may hold values from -73 to 76
- atom_types: int32 [65536], P(('gx', 'gy', 'gz')), may hold values from 0 to 63
- halo_send: int32 [27904], P(('gx', 'gy', 'gz')), may hold values from 0 to 2047, as said below
- neighbours: int32 [8192, 8], P(('gx', 'gy', 'gz')), may hold values from 0 to 364, as said below
- live_counts: int32 [8192], P(('gx', 'gy', 'gz')), may hold values from 1 to 8
- rep_coef: float32 [64], replicated, may hold values from 0.5 to 2
- disp_coef: float32 [64], replicated, may hold values from 0.2 to 1
- charge: float32 [64], replicated, may hold values from -1 to 1
- step_history: float32 [8, 3, 65536], P(None, None, ('gx', 'gy', 'gz')), may hold values from -9 to 9
- grad_history: float32 [8, 3, 65536], P(None, None, ('gx', 'gy', 'gz')), may hold values from -72 to 72, as said below
Outputs:
- new_coords: float32 [3, 65536], P(None, ('gx', 'gy', 'gz'))
- energy: float32 [], replicated
Inputs may be any that keep to these rules, and one draw needn't show every extreme that they name: `halo_send`: each of a domain's seven blocks holds distinct local atom indices, rising. `neighbours`: slot 0 of row r is r mod 256, the row's own cluster. `grad_history`: the product of each entry with the matching step_history entry is not negative, and each pair's inner product is positive.
All inputs are finite; a program needn't handle non-finite values.
Results may differ from a plain program's by a relative error of at most 0.0003.
Values sent between devices are 32-bit elements; how exact they have to be, the bound alone decides.
No kernel may reach another device: no remote copies, remote signals or barrier semaphores. Data moves between devices by JAX's collectives and lax.ppermute only.
A program may use at most 64 MiB of HBM per device.

v0:
```python
import math
import jax
import jax.numpy as jnp
from jax import lax
from jax.sharding import PartitionSpec as P

domain_side = 3.0
step_length = 0.5
axis_bits = {"gx": 4, "gy": 2, "gz": 1}
axis_component = {"gx": 0, "gy": 1, "gz": 2}


def shifted(value, axis, steps):
    count = lax.axis_size(axis)
    pairs = [(source, (source + steps) % count) for source in range(count)]
    return lax.ppermute(value, axis, pairs)


def export_sizes(atoms_local):
    face_rows = atoms_local // 8
    edge_rows = max(atoms_local // 64, 8)
    corner_rows = max(atoms_local // 512, 8)
    return [face_rows, face_rows, edge_rows, face_rows, edge_rows, edge_rows, corner_rows]


def tile_gradient(ext_pos, ext_par, neighbours, live_counts):
    highest = lax.Precision.HIGHEST
    ext_clusters = ext_pos.shape[1] // 8
    pos_tiles = ext_pos.reshape(3, ext_clusters, 8).transpose(0, 2, 1)
    par_tiles = ext_par.reshape(3, ext_clusters, 8).transpose(0, 2, 1)
    both_tiles = jnp.concatenate([pos_tiles, par_tiles], axis=0)
    cluster_rows = neighbours.shape[0]
    list_width = neighbours.shape[1]
    block_rows = math.gcd(256, cluster_rows)
    block_count = cluster_rows // block_rows
    atom_rank = jnp.arange(8, dtype=jnp.int32)
    ordered_pair = (atom_rank[:, None] < atom_rank[None, :]).astype(jnp.float32)[:, :, None]
    slot_rank = jnp.tile(jnp.arange(list_width, dtype=jnp.int32), block_rows)
    ext_ids = jnp.arange(ext_clusters, dtype=jnp.int32)

    def one_block(state_pair, block_id):
        gradient, energy = state_pair
        first_row = block_id * block_rows
        listed = neighbours.reshape(-1)
        selector = (listed[:, None] == ext_ids[None, :]).astype(jnp.float32)
        live_count = jnp.repeat(live_counts, list_width)
        home_ids = jnp.repeat(first_row + jnp.arange(block_rows, dtype=jnp.int32), list_width)
        live_mask = (slot_rank < live_count).astype(jnp.float32)
        weight = live_mask[None, None, :] * jnp.where(
            (listed == home_ids)[None, None, :], ordered_pair, 1.0
        )
        pos_home = jnp.repeat(
            lax.dynamic_slice_in_dim(pos_tiles, first_row, block_rows, 2), list_width, axis=2
        )
        par_home = jnp.repeat(
            lax.dynamic_slice_in_dim(par_tiles, first_row, block_rows, 2), list_width, axis=2
        )
        other_tiles = jnp.einsum("caj,kj->cak", both_tiles, selector, precision=highest)
        pos_other = other_tiles[:3]
        par_other = other_tiles[3:]
        offset = pos_home[:, :, None, :] - pos_other[:, None, :, :]
        dist_sq = jnp.sum(offset * offset, axis=0)
        inverse = 1.0 / (1.0 + dist_sq)
        repulse = par_home[0][:, None, :] * par_other[0][None, :, :]
        attract = par_home[1][:, None, :] * par_other[1][None, :, :]
        coulomb = par_home[2][:, None, :] * par_other[2][None, :, :]
        root_inv = jnp.sqrt(inverse)
        pair_energy = repulse * inverse * inverse - attract * inverse + coulomb * root_inv
        slope = 2.0 * repulse * inverse - attract + 0.5 * coulomb / root_inv
        factor = -2.0 * weight * slope * inverse * inverse
        push_term = factor[None] * offset
        home_grad = jnp.sum(push_term, axis=2).reshape(3, 8, block_rows, list_width).sum(axis=3)
        other_grad = -jnp.sum(push_term, axis=1)
        gradient = gradient + jnp.einsum("cak,kj->caj", other_grad, selector, precision=highest)
        current = lax.dynamic_slice_in_dim(gradient, first_row, block_rows, 2)
        gradient = lax.dynamic_update_slice_in_dim(gradient, current + home_grad, first_row, 2)
        energy = energy + jnp.sum(weight * pair_energy)
        return ((gradient, energy), None)

    initial = (jnp.zeros((3, 8, ext_clusters), jnp.float32), jnp.zeros((), jnp.float32))
    (gradient, energy), unused = lax.scan(
        one_block, initial, jnp.arange(block_count, dtype=jnp.int32)
    )
    return (gradient.transpose(0, 2, 1).reshape(3, -1), energy)


def pass_along(payload, axis_name, offset):
    if axis_name == "gx":
        return shifted(payload, "gx", offset)
    if axis_name == "gy":
        return shifted(payload, "gy", offset)
    return shifted(payload, "gz", offset)


def two_loop(cross_products, grad_dots):
    memory = cross_products.shape[0] // 2
    basis_size = 2 * memory + 1
    gram_full = jnp.zeros((basis_size, basis_size), jnp.float32)
    gram_full = (
        gram_full.at[0, 1:].set(grad_dots).at[1:, 0].set(grad_dots).at[1:, 1:].set(cross_products)
    )
    unit_rows = jnp.eye(basis_size, dtype=jnp.float32)
    inverse_sy = [1.0 / cross_products[hist_id, memory + hist_id] for hist_id in range(memory)]
    alphas = [None] * memory
    coeffs = unit_rows[0]
    for hist_id in reversed(range(memory)):
        alphas[hist_id] = inverse_sy[hist_id] * jnp.sum(gram_full[1 + hist_id] * coeffs)
        coeffs = coeffs - alphas[hist_id] * unit_rows[1 + memory + hist_id]
    scaling = (
        cross_products[memory - 1, 2 * memory - 1] / cross_products[2 * memory - 1, 2 * memory - 1]
    )
    coeffs = scaling * coeffs
    for hist_id in range(memory):
        beta_term = inverse_sy[hist_id] * jnp.sum(gram_full[1 + memory + hist_id] * coeffs)
        coeffs = coeffs + (alphas[hist_id] - beta_term) * unit_rows[1 + hist_id]
    return coeffs


def on_device(
    coords,
    anchor,
    atom_types,
    halo_send,
    neighbours,
    live_counts,
    rep_coef,
    disp_coef,
    charge,
    step_history,
    grad_history,
):
    highest = lax.Precision.HIGHEST
    atoms_local = coords.shape[1]
    size_list = export_sizes(atoms_local)
    start_list = [sum(size_list[:block_pos]) for block_pos in range(7)]
    history = jnp.concatenate([step_history, grad_history], axis=0).reshape(
        2 * step_history.shape[0], -1
    )
    type_table = jnp.stack([rep_coef, disp_coef, charge])
    type_ids = jnp.arange(type_table.shape[1], dtype=jnp.int32)
    one_hot = (atom_types[None, :] == type_ids[:, None]).astype(jnp.float32)
    params = jnp.dot(type_table, one_hot, precision=highest)
    local_rows = jnp.concatenate([coords, params], axis=0)
    exported = jnp.take(local_rows, halo_send, axis=1)
    axis_order = ["gz", "gy", "gx"]
    held_blocks = {}
    for block_code in range(1, 8):
        block_start = start_list[block_code - 1]
        held_blocks[block_code] = exported[:, block_start : block_start + size_list[block_code - 1]]
    for axis_name in axis_order:
        bit_value = axis_bits[axis_name]
        movers = [block_code for block_code in range(1, 8) if block_code & bit_value]
        payload = jnp.concatenate([held_blocks[block_code] for block_code in movers], axis=1)
        arrived = pass_along(payload, axis_name, -1)
        moved_by = jnp.array(
            [
                domain_side if component == axis_component[axis_name] else 0.0
                for component in range(6)
            ],
            jnp.float32,
        )
        arrived = arrived + moved_by[:, None]
        cursor = 0
        for block_code in movers:
            held_blocks[block_code] = arrived[:, cursor : cursor + size_list[block_code - 1]]
            cursor = cursor + size_list[block_code - 1]
    halo_part = jnp.concatenate([held_blocks[block_code] for block_code in range(1, 8)], axis=1)
    extended = jnp.concatenate([local_rows, halo_part], axis=1)
    gradient_ext, energy_local = tile_gradient(extended[:3], extended[3:], neighbours, live_counts)
    gradient = gradient_ext[:, :atoms_local]
    back_blocks = {}
    for block_code in range(1, 8):
        begin = atoms_local + start_list[block_code - 1]
        back_blocks[block_code] = gradient_ext[:, begin : begin + size_list[block_code - 1]]
    for axis_name in reversed(axis_order):
        bit_value = axis_bits[axis_name]
        movers = [block_code for block_code in range(1, 8) if block_code & bit_value]
        payload = jnp.concatenate([back_blocks[block_code] for block_code in movers], axis=1)
        arrived = pass_along(payload, axis_name, 1)
        cursor = 0
        for block_code in movers:
            back_blocks[block_code] = arrived[:, cursor : cursor + size_list[block_code - 1]]
            cursor = cursor + size_list[block_code - 1]
    returned = jnp.concatenate([back_blocks[block_code] for block_code in range(1, 8)], axis=1)
    gradient = gradient.at[:, halo_send].add(returned)
    displacement = coords - anchor
    gradient = gradient + displacement
    energy_local = energy_local + 0.5 * jnp.sum(displacement * displacement)
    flat_grad = gradient.reshape(-1)
    grad_dots_local = jnp.dot(history, flat_grad, precision=highest)
    cross_products, grad_dots, energy_sum = lax.psum(
        (jnp.dot(history, history.T, precision=highest), grad_dots_local, energy_local),
        ("gx", "gy", "gz"),
    )
    coeffs = two_loop(cross_products, grad_dots)
    basis_rows = jnp.concatenate([flat_grad[None], history], axis=0)
    direction = jnp.dot(coeffs, basis_rows, precision=highest).reshape(3, atoms_local)
    new_coords = coords - step_length * direction
    atoms_total = atoms_local * lax.axis_size("gx") * lax.axis_size("gy") * lax.axis_size("gz")
    return (new_coords, energy_sum / atoms_total)


def solution(mesh):
    placed = (
        P(None, ("gx", "gy", "gz")),
        P(None, ("gx", "gy", "gz")),
        P(("gx", "gy", "gz")),
        P(("gx", "gy", "gz")),
        P(("gx", "gy", "gz"), None),
        P(("gx", "gy", "gz")),
        P(),
        P(),
        P(),
        P(None, None, ("gx", "gy", "gz")),
        P(None, None, ("gx", "gy", "gz")),
    )
    return jax.shard_map(
        on_device,
        mesh=mesh,
        in_specs=placed,
        out_specs=(P(None, ("gx", "gy", "gz")), P()),
        check_vma=False,
    )
```

profile of v0, /device:TPU:12, one launch (start us, length us, event | category | flops | bytes accessed | tf_op | source)
XLA Modules:
  0.0 138.7 jit_solution(14454354531783564797)
XLA Ops:
  2.1 1.0 fusion.20
  4.3 1.9 %gather_fusion = f32[872,6]{1,0:T(8,128)S(1)} fusion(f32[6,2048]{0,1:T(8,128)S(1)} %copy.62, s32[1024]{0:T(1024)S(1)} %pad_clamp_fusion), kind=kCustom, calls=%fused_computation | custom fusion | bytes 45344 | tf_op jit(solution)/shard_map/jit(_take)/gather | solution.py:144
  6.7 0.9 collective-permute-start
  7.8 1.2 collective-permute-done
  9.9 1.2 convolution_bitcast_fusion
  11.1 1.9 %collective-permute-done.1 = f32[6,328]{1,0:T(8,128)S(1)} collective-permute-done((f32[6,328]{1,0:T(8,128)S(1)}, f32[6,328]{1,0:T(8,128)S(1)}, u32[]{:S(2)}, u32[]{:S(2)}) %collective-permute-start.1) | collective-permute-done | bytes 7904 | tf_op jit(solution)/shard_map/ppermute | solution.py:16
  14.8 2.2 %collective-permute-done.2 = f32[6,328]{1,0:T(8,128)S(1)} collective-permute-done((f32[6,328]{1,0:T(8,128)S(1)}, f32[6,328]{1,0:T(8,128)S(1)}, u32[]{:S(2)}, u32[]{:S(2)}) %collective-permute-start.2) | collective-permute-done | bytes 7904 | tf_op jit(solution)/shard_map/ppermute | solution.py:16
  18.3 1.2 fusion.3
  22.3 1.6 %broadcast_in_dim.99 = f32[3,8,256,8]{3,2,1,0:T(8,128)S(1)} broadcast(f32[3,8,256]{2,1,0:T(8,128)} %copy.67), dimensions={0,1,2} | broadcast | bytes 221184 | tf_op jit(solution)/shard_map/while/body/eval_jaxpr/broadcast_in_dim | solution.py:52
  24.0 2.8 %sub.111 = f32[3,8,2048]{2,1,0:T(8,128)} reshape(f32[3,8,256,8]{3,2,1,0:T(8,128)S(1)} %broadcast_in_dim.99) | data formatting | bytes 393216 | tf_op jit(solution)/shard_map/while/body/eval_jaxpr/sub | solution.py:61
  26.7 1.1 slice_bitcast_fusion.4
  30.8 1.0 fusion.18
  31.8 1.3 fusion.5
  33.1 2.7 %reshape.266 = f32[3,8,256,8]{3,2,1,0:T(8,128)S(1)} reshape(f32[3,8,2048]{2,1,0:T(8,128)} %get-tuple-element.71) | data formatting | bytes 393216 | tf_op jit(solution)/shard_map/while/body/eval_jaxpr/reshape | solution.py:72
  35.8 3.0 %fusion.1 = f32[3,8,365]{2,1,0:T(8,128)} fusion(s32[2048]{0:T(1024)S(1)} %copy-done.10, f32[3,8,2048]{2,1,0:T(8,128)} %get-tuple-element.72), kind=kOutput, calls=%fused_computation.4 | convolution fusion | flops 216082432 | bytes 239840 | tf_op jit(solution)/shard_map/while/body/eval_jaxpr/cak,kj->caj/dot_general | solution.py:74
  38.8 1.5 %reduce_sum.206 = f32[3,8,256]{2,1,0:T(8,128)} reduce(f32[3,8,256,8]{3,2,1,0:T(8,128)S(1)} %reshape.266, f32[]{:T(128)} %constant.140.clone.1), dimensions={3}, to_apply=%region_4.5 | reduce | flops 43008 | bytes 221188 | tf_op jit(solution)/shard_map/while/body/eval_jaxpr/reduce_sum | solution.py:72
  40.3 1.4 fusion.28
  41.6 1.0 copy.70
  43.0 1.8 %collective-permute-start.3 = (f32[3,328]{1,0:T(4,128)S(1)}, f32[3,328]{1,0:T(4,128)S(1)}, u32[]{:S(2)}, u32[]{:S(2)}) collective-permute-start(f32[3,328]{1,0:T(4,128)S(1)} %slice.467), channel_id=1, source_target_pairs={{0,8},{8,16},{16,24},{24,0},{1,9},{9,17},{17,25},{25,1},{2,10},{10... | collective-permute-start | bytes 11816 | tf_op jit(solution)/shard_map/ppermute | solution.py:16
  44.7 2.0 %collective-permute-done.3 = f32[3,328]{1,0:T(4,128)S(1)} collective-permute-done((f32[3,328]{1,0:T(4,128)S(1)}, f32[3,328]{1,0:T(4,128)S(1)}, u32[]{:S(2)}, u32[]{:S(2)}) %collective-permute-start.3) | collective-permute-done | bytes 3968 | tf_op jit(solution)/shard_map/ppermute | solution.py:16
  48.2 2.4 %collective-permute-done.4 = f32[3,328]{1,0:T(4,128)S(1)} collective-permute-done((f32[3,328]{1,0:T(4,128)S(1)}, f32[3,328]{1,0:T(4,128)S(1)}, u32[]{:S(2)}, u32[]{:S(2)}) %collective-permute-start.4) | collective-permute-done | bytes 3968 | tf_op jit(solution)/shard_map/ppermute | solution.py:16
  54.3 6.4 %scatter_fusion = f32[3,2048]{0,1:T(8,128)S(1)} fusion(f32[3,2048]{0,1:T(8,128)S(1)} %copy.71, s32[872]{0:T(1024)S(1)} %compare_select_fusion, f32[872,3]{1,0:T(8,128)S(1)} %copy.72), kind=kCustom, calls=%fused_computation.1 | custom fusion | flops 2616 | bytes 34880 | tf_op jit(solution)/shard_map/scatter-add | solution.py:185
  62.0 42.8 %all-reduce = (f32[16,16]{1,0:T(8,128)S(1)}, f32[16]{0:T(128)S(1)}, f32[]{:T(128)}) all-reduce(f32[16,16]{1,0:T(8,128)S(1)} %copy-done.8, f32[16]{0:T(128)S(1)} %convolution_bitcast_fusion.1, f32[]{:T(128)S(6)} %add.171), channel_id=1, replica_groups=mesh['gx'=4,'gy'=2,'gz'=4] {'gx','gy','gz'}, use_global_device_ids=true, to_apply=%region_0.1 | all-reduce | flops 273 | bytes 2184 | tf_op jit(solution)/shard_map/psum | solution.py:191
  105.5 1.6 %scatter.10 = f32[17,17]{1,0:T(8,128)S(1)} dynamic-update-slice(f32[17,17]{1,0:T(8,128)S(1)} %broadcast_in_dim.88, f32[1,16]{1,0:T(1,128)S(1)} %bitcast.102, s32[]{:T(128)} %bitcast.23, s32[]{:T(128)} %bitcast.24) | dynamic-update-slice | bytes 132 | tf_op jit(solution)/shard_map/scatter | solution.py:100
  (144 shorter events, 31.9 us)
Async XLA Ops:
  0.6 7.0 %copy-start.6 = (f32[8,3,2048]{2,0,1:T(8,128)S(1)}, f32[8,3,2048]{2,0,1:T(8,128)}, u32[]{:S(2)}) copy-start(f32[8,3,2048]{2,0,1:T(8,128)} %param.29) | copy-start | bytes 589828
  0.6 7.0 %copy-start.7 = (f32[8,3,2048]{2,0,1:T(8,128)S(1)}, f32[8,3,2048]{2,0,1:T(8,128)}, u32[]{:S(2)}) copy-start(f32[8,3,2048]{2,0,1:T(8,128)} %param.30) | copy-start | bytes 589828
  0.7 7.1 %copy-start.14 = (s32[256]{0:T(256)S(1)}, s32[256]{0:T(256)}, u32[]{:S(2)}) copy-start(s32[256]{0:T(256)} %param.25) | copy-start | bytes 3076
  3.1 6.0 %copy-start.17 = (f32[6]{0:T(128)S(1)}, f32[6]{0:T(128)}, u32[]{:S(2)}) copy-start(f32[6]{0:T(128)} %constant.151.clone) | copy-start | bytes 76
  4.3 8.8 %copy-start.16 = (f32[6]{0:T(128)S(1)}, f32[6]{0:T(128)}, u32[]{:S(2)}) copy-start(f32[6]{0:T(128)} %constant.152.clone) | copy-start | bytes 76
  4.3 9.5 %copy-start.13 = (s32[256,8]{0,1:T(8,128)S(1)}, s32[256,8]{0,1:T(8,128)}, u32[]{:S(2)}) copy-start(s32[256,8]{0,1:T(8,128)} %param.24) | copy-start | bytes 24580
  6.2 10.8 %copy-start.15 = (f32[6]{0:T(128)S(1)}, f32[6]{0:T(128)}, u32[]{:S(2)}) copy-start(f32[6]{0:T(128)} %constant.153.clone) | copy-start | bytes 76
  6.7 2.3 %collective-permute-start = (f32[6,328]{1,0:T(8,128)S(1)}, f32[6,328]{1,0:T(8,128)S(1)}, u32[]{:S(2)}, u32[]{:S(2)}) collective-permute-start(f32[6,328]{1,0:T(8,128)S(1)} %pad_maximum_fusion.1), channel_id=1, source_target_pairs={{0,3},{1,0},{2,1},{3,2},{4,7},{5,4},{6,5},{7,6},{8,11},{9,8},{10,9... | collective-permute-start | bytes 23624 | tf_op jit(solution)/shard_map/ppermute | solution.py:16
  9.4 3.7 %collective-permute-start.1 = (f32[6,328]{1,0:T(8,128)S(1)}, f32[6,328]{1,0:T(8,128)S(1)}, u32[]{:S(2)}, u32[]{:S(2)}) collective-permute-start(f32[6,328]{1,0:T(8,128)S(1)} %pad_maximum_fusion.2), channel_id=1, source_target_pairs={{0,4},{4,0},{1,5},{5,1},{2,6},{6,2},{3,7},{7,3},{8,12},{12,8},{9,1... | collective-permute-start | bytes 23624 | tf_op jit(solution)/shard_map/ppermute | solution.py:16
  13.3 3.7 %collective-permute-start.2 = (f32[6,328]{1,0:T(8,128)S(1)}, f32[6,328]{1,0:T(8,128)S(1)}, u32[]{:S(2)}, u32[]{:S(2)}) collective-permute-start(f32[6,328]{1,0:T(8,128)S(1)} %pad_maximum_fusion.3), channel_id=1, source_target_pairs={{0,24},{8,0},{16,8},{24,16},{1,25},{9,1},{17,9},{25,17},{2,26},{10... | collective-permute-start | bytes 23624 | tf_op jit(solution)/shard_map/ppermute | solution.py:16
  14.0 4.3 %copy-start.9 = (s32[2048]{0:T(1024)}, s32[2048]{0:T(1024)S(1)}, u32[]{:S(2)}) copy-start(s32[2048]{0:T(1024)S(1)} %reshape.262) | copy-start | bytes 24580
  29.1 1.5 %copy-start = (f32[3,8,2048]{2,1,0:T(8,128)S(1)}, f32[3,8,2048]{2,1,0:T(8,128)}, u32[]{:S(2)}) copy-start(f32[3,8,2048]{2,1,0:T(8,128)} %slice.459) | copy-start | bytes 589828
  29.1 1.5 %copy-start.1 = (f32[3,8,2048]{2,1,0:T(8,128)S(1)}, f32[3,8,2048]{2,1,0:T(8,128)}, u32[]{:S(2)}) copy-start(f32[3,8,2048]{2,1,0:T(8,128)} %sub.111) | copy-start | bytes 589828
  29.7 1.1 copy-start.3
  29.7 1.1 copy-start.4
  29.7 1.1 copy-start.5
  29.7 1.1 copy-start.12
  33.1 2.7 %copy-start.10 = (s32[2048]{0:T(1024)S(1)}, s32[2048]{0:T(1024)}, u32[]{:S(2)}) copy-start(s32[2048]{0:T(1024)} %copy-done.9) | copy-start | bytes 24580
  40.2 10.5 %copy-start.2 = (f32[3,2048]{1,0:T(4,128)S(1)}, f32[3,2048]{1,0:T(4,128)}, u32[]{:S(2)}) copy-start(f32[3,2048]{1,0:T(4,128)} %param.20) | copy-start | bytes 73732
  40.2 10.6 %copy-start.11 = (f32[3,2048]{1,0:T(4,128)S(1)}, f32[3,2048]{1,0:T(4,128)}, u32[]{:S(2)}) copy-start(f32[3,2048]{1,0:T(4,128)} %param.21) | copy-start | bytes 73732
  43.0 3.8 %collective-permute-start.3 = (f32[3,328]{1,0:T(4,128)S(1)}, f32[3,328]{1,0:T(4,128)S(1)}, u32[]{:S(2)}, u32[]{:S(2)}) collective-permute-start(f32[3,328]{1,0:T(4,128)S(1)} %slice.467), channel_id=1, source_target_pairs={{0,8},{8,16},{16,24},{24,0},{1,9},{9,17},{17,25},{25,1},{2,10},{10... | collective-permute-start | bytes 11816 | tf_op jit(solution)/shard_map/ppermute | solution.py:16
  46.9 3.6 %collective-permute-start.4 = (f32[3,328]{1,0:T(4,128)S(1)}, f32[3,328]{1,0:T(4,128)S(1)}, u32[]{:S(2)}, u32[]{:S(2)}) collective-permute-start(f32[3,328]{1,0:T(4,128)S(1)} %pad_maximum_fusion.4), channel_id=1, source_target_pairs={{0,4},{4,0},{1,5},{5,1},{2,6},{6,2},{3,7},{7,3},{8,12},{12,8},{9,1... | collective-permute-start | bytes 11816 | tf_op jit(solution)/shard_map/ppermute | solution.py:16
  50.8 3.1 %collective-permute-start.5 = (f32[3,328]{1,0:T(4,128)S(1)}, f32[3,328]{1,0:T(4,128)S(1)}, u32[]{:S(2)}, u32[]{:S(2)}) collective-permute-start(f32[3,328]{1,0:T(4,128)S(1)} %pad_maximum_fusion.5), channel_id=1, source_target_pairs={{0,1},{1,2},{2,3},{3,0},{4,5},{5,6},{6,7},{7,4},{8,9},{9,10},{10,1... | collective-permute-start | bytes 11816 | tf_op jit(solution)/shard_map/ppermute | solution.py:16
  54.1 7.9 %copy-start.8 = (f32[16,16]{1,0:T(8,128)S(1)}, f32[16,16]{1,0:T(8,128)}, u32[]{:S(2)}) copy-start(f32[16,16]{1,0:T(8,128)} %convolution_bitcast_fusion) | copy-start | bytes 3076
where the time goes:
time: 140 us; the launch traced here: 139 us
  blocking collectives  42.8 us (31%)
  other arithmetic  26.8 us (19%)
  local copies, waits for them, and re-layouts  25.8 us (18%)
  between operations  20.9 us (15%)
  waiting for transfers between devices  10.5 us (8%)
  matrix products  7.65 us (5%)
  starting transfers between devices  4.16 us (3%)
    psum x1, blocking collectives, on_device(): lax.psum((jnp.dot(history, history.T, precision=highest), grad_dots_local...  42.8 us
    ppermute x6, waiting for transfers between devices, shifted(): return lax.ppermute(value, axis, pairs)  10.5 us
    scatter-add x1, other arithmetic, on_device(): gradient = gradient.at[:, halo_send].add(returned)  6.44 us
    reduce_sum x8, other arithmetic, two_loop(): jnp.sum(gram_full[1 + memory + hist_id] * coeffs)  5.12 us
    reduce_sum x8, other arithmetic, two_loop(): jnp.sum(gram_full[1 + hist_id] * coeffs)  5.11 us
    ppermute x6, starting transfers between devices, shifted(): return lax.ppermute(value, axis, pairs)  4.16 us
    dot_general x1, matrix products, one_block(): jnp.einsum('cak,kj->caj', other_grad, selector, precision=highest)  2.95 us
  transfers between devices with their start and end apart: 6, of which 6 were waited for; matrix products, arithmetic and copies ran while one was open for 3% of the time, Pallas kernels for 0%

commit v1 on v0

--- a/solution.py
+++ b/solution.py
@@ -188,9 +188,14 @@
     energy_local = energy_local + 0.5 * jnp.sum(displacement * displacement)
     flat_grad = gradient.reshape(-1)
     grad_dots_local = jnp.dot(history, flat_grad, precision=highest)
-    cross_products, grad_dots, energy_sum = lax.psum(
-        (jnp.dot(history, history.T, precision=highest), grad_dots_local, energy_local),
-        ("gx", "gy", "gz"),
+
+    def point_the_signs(x_in):
+        for t in (("gy", "gz"), "gx"):
+            x_in = lax.psum(x_in, axis_name=t)
+        return x_in
+
+    cross_products, grad_dots, energy_sum = point_the_signs(
+        (jnp.dot(history, history.T, precision=highest), grad_dots_local, energy_local)
     )
     coeffs = two_loop(cross_products, grad_dots)
     basis_rows = jnp.concatenate([flat_grad[None], history], axis=0)

time: 140 us -> 128 us (0.914)
  the two profiles are of different devices: /device:TPU:12 before, /device:TPU:0 now
where the time goes in v1:
time: 128 us; the launch traced here: 127 us
  other arithmetic  26.8 us (21%)
  blocking collectives  26.1 us (20%)
  local copies, waits for them, and re-layouts  25.8 us (20%)
  between operations  20.9 us (16%)
  waiting for transfers between devices  10 us (8%)
  starting transfers between devices  9.5 us (7%)
  matrix products  7.65 us (6%)
    psum x2, blocking collectives, point_the_signs(): x_in = lax.psum(x_in, axis_name=t)  26.1 us
    ppermute x6, waiting for transfers between devices, shifted(): return lax.ppermute(value, axis, pairs)  10 us
    ppermute x6, starting transfers between devices, shifted(): return lax.ppermute(value, axis, pairs)  9.5 us
    scatter-add x1, other arithmetic, on_device(): gradient = gradient.at[:, halo_send].add(returned)  6.44 us
    reduce_sum x8, other arithmetic, two_loop(): jnp.sum(gram_full[1 + memory + hist_id] * coeffs)  5.12 us
    reduce_sum x8, other arithmetic, two_loop(): jnp.sum(gram_full[1 + hist_id] * coeffs)  5.11 us
    dot_general x1, matrix products, one_block(): jnp.einsum('cak,kj->caj', other_grad, selector, precision=highest)  2.95 us
    sub x1, local copies, waits for them, and re-layouts, one_block(): offset = pos_home[:, :, None, :] - pos_other[:, None, :, :]  2.76 us
  transfers between devices with their start and end apart: 6, of which 6 were waited for; matrix products, arithmetic and copies ran while one was open for 3% of the time, Pallas kernels for 0%

profile of v1, /device:TPU:0, one launch (start us, length us, event | category | flops | bytes accessed | tf_op | source)
XLA Modules:
  0.0 126.8 jit_solution(4249474000943316165)
XLA Ops:
  2.1 1.0 fusion.20
  4.3 1.9 %gather_fusion = f32[872,6]{1,0:T(8,128)S(1)} fusion(f32[6,2048]{0,1:T(8,128)S(1)} %copy.62, s32[1024]{0:T(1024)S(1)} %pad_clamp_fusion), kind=kCustom, calls=%fused_computation | custom fusion | bytes 45344 | tf_op jit(solution)/shard_map/jit(_take)/gather | solution.py:144
  6.7 2.4 %collective-permute-start = (f32[6,328]{1,0:T(8,128)S(1)}, f32[6,328]{1,0:T(8,128)S(1)}, u32[]{:S(2)}, u32[]{:S(2)}) collective-permute-start(f32[6,328]{1,0:T(8,128)S(1)} %pad_maximum_fusion.1), channel_id=1, source_target_pairs={{0,3},{1,0},{2,1},{3,2},{4,7},{5,4},{6,5},{7,6},{8,11},{9,8},{10,9... | collective-permute-start | bytes 23624 | tf_op jit(solution)/shard_map/ppermute | solution.py:16
  9.3 1.2 collective-permute-done
  10.8 1.5 %collective-permute-start.1 = (f32[6,328]{1,0:T(8,128)S(1)}, f32[6,328]{1,0:T(8,128)S(1)}, u32[]{:S(2)}, u32[]{:S(2)}) collective-permute-start(f32[6,328]{1,0:T(8,128)S(1)} %pad_maximum_fusion.2), channel_id=1, source_target_pairs={{0,4},{4,0},{1,5},{5,1},{2,6},{6,2},{3,7},{7,3},{8,12},{12,8},{9,1... | collective-permute-start | bytes 23624 | tf_op jit(solution)/shard_map/ppermute | solution.py:16
  12.4 1.2 convolution_bitcast_fusion
  14.8 3.6 %collective-permute-start.2 = (f32[6,328]{1,0:T(8,128)S(1)}, f32[6,328]{1,0:T(8,128)S(1)}, u32[]{:S(2)}, u32[]{:S(2)}) collective-permute-start(f32[6,328]{1,0:T(8,128)S(1)} %pad_maximum_fusion.3), channel_id=1, source_target_pairs={{0,24},{8,0},{16,8},{24,16},{1,25},{9,1},{17,9},{25,17},{2,26},{10... | collective-permute-start | bytes 23624 | tf_op jit(solution)/shard_map/ppermute | solution.py:16
  21.1 1.2 fusion.3
  25.1 1.6 %broadcast_in_dim.99 = f32[3,8,256,8]{3,2,1,0:T(8,128)S(1)} broadcast(f32[3,8,256]{2,1,0:T(8,128)} %copy.67), dimensions={0,1,2} | broadcast | bytes 221184 | tf_op jit(solution)/shard_map/while/body/eval_jaxpr/broadcast_in_dim | solution.py:52
  26.7 2.8 %sub.111 = f32[3,8,2048]{2,1,0:T(8,128)} reshape(f32[3,8,256,8]{3,2,1,0:T(8,128)S(1)} %broadcast_in_dim.99) | data formatting | bytes 393216 | tf_op jit(solution)/shard_map/while/body/eval_jaxpr/sub | solution.py:61
  29.5 1.1 slice_bitcast_fusion.4
  33.6 1.0 fusion.18
  34.6 1.3 fusion.5
  35.9 2.7 %reshape.266 = f32[3,8,256,8]{3,2,1,0:T(8,128)S(1)} reshape(f32[3,8,2048]{2,1,0:T(8,128)} %get-tuple-element.71) | data formatting | bytes 393216 | tf_op jit(solution)/shard_map/while/body/eval_jaxpr/reshape | solution.py:72
  38.6 3.0 %fusion.1 = f32[3,8,365]{2,1,0:T(8,128)} fusion(s32[2048]{0:T(1024)S(1)} %copy-done.10, f32[3,8,2048]{2,1,0:T(8,128)} %get-tuple-element.72), kind=kOutput, calls=%fused_computation.4 | convolution fusion | flops 216082432 | bytes 239840 | tf_op jit(solution)/shard_map/while/body/eval_jaxpr/cak,kj->caj/dot_general | solution.py:74
  41.5 1.5 %reduce_sum.206 = f32[3,8,256]{2,1,0:T(8,128)} reduce(f32[3,8,256,8]{3,2,1,0:T(8,128)S(1)} %reshape.266, f32[]{:T(128)} %constant.140.clone.1), dimensions={3}, to_apply=%region_5.6 | reduce | flops 43008 | bytes 221188 | tf_op jit(solution)/shard_map/while/body/eval_jaxpr/reduce_sum | solution.py:72
  43.0 1.4 %fusion.28 = f32[3,8,365]{2,1,0:T(8,128)} fusion(f32[3,8,365]{2,1,0:T(8,128)} %fusion.1, f32[3,8,256]{2,1,0:T(8,128)} %reduce_sum.206), kind=kLoop, calls=%fused_computation.59 | loop fusion | flops 6144 | bytes 73728 | tf_op jit(solution)/shard_map/while/body/eval_jaxpr/dynamic_update_slice | solution.py:76
  46.2 5.4 %collective-permute-done.3 = f32[3,328]{1,0:T(4,128)S(1)} collective-permute-done((f32[3,328]{1,0:T(4,128)S(1)}, f32[3,328]{1,0:T(4,128)S(1)}, u32[]{:S(2)}, u32[]{:S(2)}) %collective-permute-start.3) | collective-permute-done | bytes 3968 | tf_op jit(solution)/shard_map/ppermute | solution.py:16
  51.8 1.5 %collective-permute-start.4 = (f32[3,328]{1,0:T(4,128)S(1)}, f32[3,328]{1,0:T(4,128)S(1)}, u32[]{:S(2)}, u32[]{:S(2)}) collective-permute-start(f32[3,328]{1,0:T(4,128)S(1)} %pad_maximum_fusion.4), channel_id=1, source_target_pairs={{0,4},{4,0},{1,5},{5,1},{2,6},{6,2},{3,7},{7,3},{8,12},{12,8},{9,1... | collective-permute-start | bytes 11816 | tf_op jit(solution)/shard_map/ppermute | solution.py:16
  54.0 1.4 %collective-permute-done.4 = f32[3,328]{1,0:T(4,128)S(1)} collective-permute-done((f32[3,328]{1,0:T(4,128)S(1)}, f32[3,328]{1,0:T(4,128)S(1)}, u32[]{:S(2)}, u32[]{:S(2)}) %collective-permute-start.4) | collective-permute-done | bytes 3968 | tf_op jit(solution)/shard_map/ppermute | solution.py:16
  59.2 6.4 %scatter_fusion = f32[3,2048]{0,1:T(8,128)S(1)} fusion(f32[3,2048]{0,1:T(8,128)S(1)} %copy.71, s32[872]{0:T(1024)S(1)} %compare_select_fusion, f32[872,3]{1,0:T(8,128)S(1)} %copy.72), kind=kCustom, calls=%fused_computation.1 | custom fusion | flops 2616 | bytes 34880 | tf_op jit(solution)/shard_map/scatter-add | solution.py:185
  66.9 14.8 %all-reduce = (f32[16,16]{1,0:T(8,128)S(1)}, f32[16]{0:T(128)S(1)}, f32[]{:T(128)}) all-reduce(f32[16,16]{1,0:T(8,128)S(1)} %copy-done.8, f32[16]{0:T(128)S(1)} %convolution_bitcast_fusion.1, f32[]{:T(128)S(6)} %add.177), channel_id=1, replica_groups=mesh['gx'=4,'gy'=2,'gz'=4] {'gy','gz'}, use_global_device_ids=true, to_apply=%region_0.1 | all-reduce | flops 273 | bytes 2184 | tf_op jit(solution)/shard_map/psum | solution.py:194
  81.6 11.3 %all-reduce.1 = (f32[16,16]{1,0:T(8,128)S(1)}, f32[16]{0:T(128)S(1)}, f32[]{:T(128)}) all-reduce(f32[16,16]{1,0:T(8,128)S(1)} %get-tuple-element.73, f32[16]{0:T(128)S(1)} %get-tuple-element.74, f32[]{:T(128)} %get-tuple-element.75), channel_id=1, replica_groups=mesh['gx'=4,'gy'=2,'gz'=4] {'gx'}, use_global_device_ids=true, to_apply=%region_1.2 | all-reduce | flops 273 | bytes 2184 | tf_op jit(solution)/shard_map/psum | solution.py:194
  93.7 1.6 %scatter.10 = f32[17,17]{1,0:T(8,128)S(1)} dynamic-update-slice(f32[17,17]{1,0:T(8,128)S(1)} %broadcast_in_dim.88, f32[1,16]{1,0:T(1,128)S(1)} %bitcast.102, s32[]{:T(128)} %bitcast.23, s32[]{:T(128)} %bitcast.24) | dynamic-update-slice | bytes 132 | tf_op jit(solution)/shard_map/scatter | solution.py:100
  (145 shorter events, 33.2 us)
Async XLA Ops:
  0.6 8.5 %copy-start.6 = (f32[8,3,2048]{2,0,1:T(8,128)S(1)}, f32[8,3,2048]{2,0,1:T(8,128)}, u32[]{:S(2)}) copy-start(f32[8,3,2048]{2,0,1:T(8,128)} %param.29) | copy-start | bytes 589828
  0.6 8.5 %copy-start.7 = (f32[8,3,2048]{2,0,1:T(8,128)S(1)}, f32[8,3,2048]{2,0,1:T(8,128)}, u32[]{:S(2)}) copy-start(f32[8,3,2048]{2,0,1:T(8,128)} %param.30) | copy-start | bytes 589828
  0.7 8.5 %copy-start.14 = (s32[256]{0:T(256)S(1)}, s32[256]{0:T(256)}, u32[]{:S(2)}) copy-start(s32[256]{0:T(256)} %param.25) | copy-start | bytes 3076
  3.1 7.4 %copy-start.17 = (f32[6]{0:T(128)S(1)}, f32[6]{0:T(128)}, u32[]{:S(2)}) copy-start(f32[6]{0:T(128)} %constant.151.clone) | copy-start | bytes 76
  4.3 10.3 %copy-start.16 = (f32[6]{0:T(128)S(1)}, f32[6]{0:T(128)}, u32[]{:S(2)}) copy-start(f32[6]{0:T(128)} %constant.152.clone) | copy-start | bytes 76
  4.3 14.1 %copy-start.13 = (s32[256,8]{0,1:T(8,128)S(1)}, s32[256,8]{0,1:T(8,128)}, u32[]{:S(2)}) copy-start(s32[256,8]{0,1:T(8,128)} %param.24) | copy-start | bytes 24580
  6.2 13.6 %copy-start.15 = (f32[6]{0:T(128)S(1)}, f32[6]{0:T(128)}, u32[]{:S(2)}) copy-start(f32[6]{0:T(128)} %constant.153.clone) | copy-start | bytes 76
  6.7 3.8 %collective-permute-start = (f32[6,328]{1,0:T(8,128)S(1)}, f32[6,328]{1,0:T(8,128)S(1)}, u32[]{:S(2)}, u32[]{:S(2)}) collective-permute-start(f32[6,328]{1,0:T(8,128)S(1)} %pad_maximum_fusion.1), channel_id=1, source_target_pairs={{0,3},{1,0},{2,1},{3,2},{4,7},{5,4},{6,5},{7,6},{8,11},{9,8},{10,9... | collective-permute-start | bytes 23624 | tf_op jit(solution)/shard_map/ppermute | solution.py:16
  10.8 3.7 %collective-permute-start.1 = (f32[6,328]{1,0:T(8,128)S(1)}, f32[6,328]{1,0:T(8,128)S(1)}, u32[]{:S(2)}, u32[]{:S(2)}) collective-permute-start(f32[6,328]{1,0:T(8,128)S(1)} %pad_maximum_fusion.2), channel_id=1, source_target_pairs={{0,4},{4,0},{1,5},{5,1},{2,6},{6,2},{3,7},{7,3},{8,12},{12,8},{9,1... | collective-permute-start | bytes 23624 | tf_op jit(solution)/shard_map/ppermute | solution.py:16
  14.8 5.0 %collective-permute-start.2 = (f32[6,328]{1,0:T(8,128)S(1)}, f32[6,328]{1,0:T(8,128)S(1)}, u32[]{:S(2)}, u32[]{:S(2)}) collective-permute-start(f32[6,328]{1,0:T(8,128)S(1)} %pad_maximum_fusion.3), channel_id=1, source_target_pairs={{0,24},{8,0},{16,8},{24,16},{1,25},{9,1},{17,9},{25,17},{2,26},{10... | collective-permute-start | bytes 23624 | tf_op jit(solution)/shard_map/ppermute | solution.py:16
  18.6 2.4 %copy-start.9 = (s32[2048]{0:T(1024)}, s32[2048]{0:T(1024)S(1)}, u32[]{:S(2)}) copy-start(s32[2048]{0:T(1024)S(1)} %reshape.262) | copy-start | bytes 24580
  31.9 1.5 %copy-start = (f32[3,8,2048]{2,1,0:T(8,128)S(1)}, f32[3,8,2048]{2,1,0:T(8,128)}, u32[]{:S(2)}) copy-start(f32[3,8,2048]{2,1,0:T(8,128)} %slice.459) | copy-start | bytes 589828
  31.9 1.5 %copy-start.1 = (f32[3,8,2048]{2,1,0:T(8,128)S(1)}, f32[3,8,2048]{2,1,0:T(8,128)}, u32[]{:S(2)}) copy-start(f32[3,8,2048]{2,1,0:T(8,128)} %sub.111) | copy-start | bytes 589828
  32.5 1.1 copy-start.3
  32.5 1.1 copy-start.4
  32.5 1.1 copy-start.5
  32.5 1.1 copy-start.12
  35.9 2.7 %copy-start.10 = (s32[2048]{0:T(1024)S(1)}, s32[2048]{0:T(1024)}, u32[]{:S(2)}) copy-start(s32[2048]{0:T(1024)} %copy-done.9) | copy-start | bytes 24580
  43.0 12.6 %copy-start.2 = (f32[3,2048]{1,0:T(4,128)S(1)}, f32[3,2048]{1,0:T(4,128)}, u32[]{:S(2)}) copy-start(f32[3,2048]{1,0:T(4,128)} %param.20) | copy-start | bytes 73732
  43.0 12.6 %copy-start.11 = (f32[3,2048]{1,0:T(4,128)S(1)}, f32[3,2048]{1,0:T(4,128)}, u32[]{:S(2)}) copy-start(f32[3,2048]{1,0:T(4,128)} %param.21) | copy-start | bytes 73732
  45.8 5.9 %collective-permute-start.3 = (f32[3,328]{1,0:T(4,128)S(1)}, f32[3,328]{1,0:T(4,128)S(1)}, u32[]{:S(2)}, u32[]{:S(2)}) collective-permute-start(f32[3,328]{1,0:T(4,128)S(1)} %slice.467), channel_id=1, source_target_pairs={{0,8},{8,16},{16,24},{24,0},{1,9},{9,17},{17,25},{25,1},{2,10},{10... | collective-permute-start | bytes 11816 | tf_op jit(solution)/shard_map/ppermute | solution.py:16
  51.8 3.6 %collective-permute-start.4 = (f32[3,328]{1,0:T(4,128)S(1)}, f32[3,328]{1,0:T(4,128)S(1)}, u32[]{:S(2)}, u32[]{:S(2)}) collective-permute-start(f32[3,328]{1,0:T(4,128)S(1)} %pad_maximum_fusion.4), channel_id=1, source_target_pairs={{0,4},{4,0},{1,5},{5,1},{2,6},{6,2},{3,7},{7,3},{8,12},{12,8},{9,1... | collective-permute-start | bytes 11816 | tf_op jit(solution)/shard_map/ppermute | solution.py:16
  55.6 3.1 %collective-permute-start.5 = (f32[3,328]{1,0:T(4,128)S(1)}, f32[3,328]{1,0:T(4,128)S(1)}, u32[]{:S(2)}, u32[]{:S(2)}) collective-permute-start(f32[3,328]{1,0:T(4,128)S(1)} %pad_maximum_fusion.5), channel_id=1, source_target_pairs={{0,1},{1,2},{2,3},{3,0},{4,5},{5,6},{6,7},{7,4},{8,9},{9,10},{10,1... | collective-permute-start | bytes 11816 | tf_op jit(solution)/shard_map/ppermute | solution.py:16
  58.9 7.9 %copy-start.8 = (f32[16,16]{1,0:T(8,128)S(1)}, f32[16,16]{1,0:T(8,128)}, u32[]{:S(2)}) copy-start(f32[16,16]{1,0:T(8,128)} %convolution_bitcast_fusion) | copy-start | bytes 3076
